TPU v7x, 32 devices: a whole 2x2x4 slice. The times are simulated.
32 devices in a mesh: grp: 1, sp: 4 (over z), blk: 4 (over y, x), rep: 2 (over core).
Axes of the slice: x: 2, y: 2, z: 4, core: 2. Of those that a mesh axis runs over, the one named last changes fastest.
Arguments:
- hidden: bfloat16 [4, 512, 4096], P(('grp', 'blk'), 'sp'), may hold values from -64 to 64
- queries: bfloat16 [4, 512, 4096], P(('grp', 'blk'), 'sp', 'rep'), may hold values from -600 to 600
- norm_gain: float32 [4096], replicated, may hold values from 0.1 to 1.9
- key_matrix: bfloat16 [4096, 1024], P('sp', 'rep'), may hold values from -0.09375 to 0.09375
- value_matrix: bfloat16 [4096, 1024], P('sp', 'rep'), may hold values from -0.09375 to 0.09375
- key_shift_bias: bfloat16 [1024], P('rep'), may hold values from -3 to 3
- value_shift_bias: bfloat16 [1024], P('rep'), may hold values from -3 to 3
- doc_lengths: int32 [8], P('grp'), may hold values from 1 to 1025, 2048 in all
Outputs:
- attended: bfloat16 [4, 512, 4096], P(('grp', 'blk'), 'sp', 'rep')
Inputs may be any that keep to these rules, and one draw needn't show every extreme that they name: `doc_lengths`: the lengths of the 8 documents packed in order into the sequence; they sum to 2048, and the longest is exactly 1025 tokens.
All inputs are finite; a program needn't handle non-finite values.
Results may differ from a plain program's by a relative error of at most 0.012.
The roundings to bfloat16 on the way count: a program that leaves them out, or rounds other values in their place, can miss the bound.
Values may be sent and summed in bfloat16 or wider, within the bound.
A program may use at most 64 MiB of HBM per device.

v0:
```python
import functools
import math

import jax
import jax.numpy as jnp
from jax import lax
from jax.experimental import pallas as pl
from jax.experimental.pallas import tpu as pltpu
from jax.sharding import PartitionSpec as P

HEAD = 128
EPS_VALUE = 1e-06
THETA_BASE = 1000000.0
NEG_FILL = -1e30
MESH = pl.DeviceIdType.MESH
F32, BF16 = jnp.float32, jnp.bfloat16


def kernel(
    sizes,
    hidden_ref,
    queries_ref,
    gain_ref,
    kw_ref,
    vw_ref,
    kb_ref,
    vb_ref,
    docs_ref,
    out_ref,
    hid,
    wts,
    normed,
    feats,
    part_own,
    part_out,
    pair_in,
    pair_out,
    part_in,
    kv,
    qbuf,
    obuf,
    cos_buf,
    sin_buf,
    mask_buf,
    load_sem,
    feat_send,
    feat_recv,
    fwd_send,
    fwd_recv,
    q_send,
    q_recv,
    pair_send,
    pair_recv,
    part_send,
    part_recv,
    kv_send,
    kv_recv,
    o_send,
    o_recv,
):
    sp, blks, reps, rows = sizes
    me = lax.axis_index("sp")
    blk = lax.axis_index("blk")
    rep = lax.axis_index("rep")
    half = rows // reps
    span = sp * rows
    fs = kw_ref.shape[0]
    kv_heads = kw_ref.shape[1] // HEAD
    fold = sp // kv_heads
    my_head = me // fold
    q_cols = queries_ref.shape[2] // sp
    heads = q_cols // HEAD
    window = 2 * span + rows
    docs = docs_ref.shape[0]

    pairs = sp // 2
    my_pair = me // 2
    parity = lax.rem(me, 2)
    slots = pair_in.shape[0]

    def place(k):
        pair = lax.rem(my_pair + k // 2, pairs)
        return 2 * pair + lax.rem(parity + lax.rem(k, 2), 2)

    peer = place
    partner = place(1)

    def slot_head(slot, side):
        return slot if fold > 1 else 2 * slot + side

    barrier = pltpu.get_barrier_semaphore()
    for k in range(1, sp):
        pl.semaphore_signal(barrier, inc=1, device_id={"sp": peer(k)}, device_id_type=MESH)
    for k in range(1, reps):
        pl.semaphore_signal(
            barrier, inc=1, device_id={"rep": lax.rem(rep + k, reps)}, device_id_type=MESH
        )
    for dist in (1, 2):
        pl.semaphore_signal(
            barrier, inc=1, device_id={"blk": lax.rem(blk + dist, blks)}, device_id_type=MESH
        )
        pl.semaphore_signal(
            barrier, inc=1, device_id={"blk": lax.rem(blk + blks - dist, blks)}, device_id_type=MESH
        )

    load_hid = pltpu.make_async_copy(
        hidden_ref.at[0, pl.ds(pl.multiple_of(rep * half, half), half)], hid, load_sem.at[0]
    )
    load_k = pltpu.make_async_copy(kw_ref, wts.at[:, : kv_heads * HEAD], load_sem.at[1])
    load_v = pltpu.make_async_copy(vw_ref, wts.at[:, kv_heads * HEAD :], load_sem.at[2])
    load_q = pltpu.make_async_copy(
        queries_ref.at[0, :, pl.ds(pl.multiple_of(me * q_cols, q_cols), q_cols)],
        qbuf.at[me],
        load_sem.at[3],
    )
    load_hid.start()
    load_k.start()
    load_v.start()
    load_q.start()

    load_hid.wait()
    values = hid[...].astype(F32)
    scale = lax.rsqrt(jnp.mean(values * values, axis=1, keepdims=True) + EPS_VALUE)
    for d in range(sp):
        cols = slice(d * fs, (d + 1) * fs)
        normed[d] = (hid[:, cols].astype(F32) * scale * gain_ref[:, cols]).astype(BF16)

    pl.semaphore_wait(barrier, sp - 1 + reps - 1 + 4)

    def feat_copy(k):
        d = peer(k)
        return pltpu.make_async_remote_copy(
            src_ref=normed.at[d],
            dst_ref=feats.at[me, rep],
            send_sem=feat_send.at[d],
            recv_sem=feat_recv.at[me],
            device_id={"sp": d},
            device_id_type=MESH,
        )

    def feat_arrival(s):
        return pltpu.make_async_remote_copy(
            src_ref=normed.at[0],
            dst_ref=feats.at[s, rep],
            send_sem=feat_send.at[0],
            recv_sem=feat_recv.at[s],
            device_id={"sp": s},
            device_id_type=MESH,
        )

    other = lax.rem(rep + 1, reps)

    def fwd_copy(s, source):
        return pltpu.make_async_remote_copy(
            src_ref=source,
            dst_ref=feats.at[s, rep],
            send_sem=fwd_send.at[s],
            recv_sem=fwd_recv.at[s],
            device_id={"rep": other},
            device_id_type=MESH,
        )

    def fwd_arrival(s):
        return pltpu.make_async_remote_copy(
            src_ref=normed.at[0],
            dst_ref=feats.at[s, other],
            send_sem=fwd_send.at[s],
            recv_sem=fwd_recv.at[s],
            device_id={"rep": other},
            device_id_type=MESH,
        )

    order = list(range(1, sp))
    for k in order:
        feat_copy(k).start()
    fwd_copy(me, normed.at[me]).start()
    feats[me, rep] = normed[me]

    token_base = blk * span
    lanes = lax.broadcasted_iota(jnp.int32, (1, HEAD), 1)
    index = lax.rem(lanes, HEAD // 2).astype(F32)
    inverse = jnp.exp(index * (-2.0 * math.log(THETA_BASE) / HEAD))
    sign = jnp.where(lanes < HEAD // 2, -1.0, 1.0)

    def angle_step(j, carry):
        at = pl.ds(pl.multiple_of(j * rows, rows), rows)
        places = token_base + j * rows + lax.broadcasted_iota(jnp.int32, (rows, HEAD), 0)
        angles = places.astype(F32) * inverse
        cos_buf[at, :] = jnp.cos(angles)
        sin_buf[at, :] = jnp.sin(angles) * sign
        return carry

    lax.fori_loop(0, sp, angle_step, 0)
    load_k.wait()
    load_v.wait()

    def rows_of(j):
        return pl.ds(pl.multiple_of(j * rows, rows), rows)

    def pair_copy(slot, j):
        return pltpu.make_async_remote_copy(
            src_ref=part_out.at[slot_head(slot, 1 - parity), rows_of(j)],
            dst_ref=pair_in.at[slot, rows_of(j)],
            send_sem=pair_send.at[slot],
            recv_sem=pair_recv.at[slot, j],
            device_id={"sp": partner},
            device_id_type=MESH,
        )

    def part_copy(d, j):
        slot = d // fold if fold > 1 else d // 2
        return pltpu.make_async_remote_copy(
            src_ref=pair_out.at[slot, rows_of(j)],
            dst_ref=part_in.at[my_pair, rows_of(j)],
            send_sem=part_send.at[d // 2],
            recv_sem=part_recv.at[my_pair, j],
            device_id={"sp": d},
            device_id_type=MESH,
        )

    def far(k):
        return 2 * lax.rem(my_pair + k, pairs) + parity

    def project(j):
        at = rows_of(j)
        block = feats[j].reshape(rows, fs)
        partial = jnp.dot(block, wts[...], preferred_element_type=F32)
        for h in range(kv_heads):
            key_part = partial[:, h * HEAD : (h + 1) * HEAD]
            value_part = partial[:, (kv_heads + h) * HEAD : (kv_heads + h + 1) * HEAD]
            part_own[h, at, :HEAD] = key_part
            part_own[h, at, HEAD:] = value_part
            part_out[h, at, :HEAD] = key_part.astype(BF16)
            part_out[h, at, HEAD:] = value_part.astype(BF16)
        for slot in range(slots):
            pair_copy(slot, j).start()

    def cross(j):
        at = rows_of(j)
        for slot in range(slots):
            pair_copy(slot, j).wait_recv()
            both = part_own[slot_head(slot, parity), at, :] + pair_in[slot, at, :].astype(F32)
            part_own[slot_head(slot, parity), at, :] = both
            pair_out[slot, at, :] = both.astype(BF16)
        for k in range(1, pairs):
            part_copy(far(k), j).start()

    fwd_arrival(me).wait_recv()
    project(me)

    def arrive(k, carry):
        s = place(k)
        feat_arrival(s).wait_recv()
        fwd_copy(s, feats.at[s, rep]).start()
        fwd_arrival(s).wait_recv()
        project(s)
        cross(place(k - 1))
        return carry

    lax.fori_loop(1, sp, arrive, 0)
    cross(place(sp - 1))

    def q_copy(d):
        return pltpu.make_async_remote_copy(
            src_ref=queries_ref.at[0, :, pl.ds(pl.multiple_of(d * q_cols, q_cols), q_cols)],
            dst_ref=qbuf.at[me],
            send_sem=q_send.at[d],
            recv_sem=q_recv.at[me],
            device_id={"sp": d},
            device_id_type=MESH,
        )

    def q_arrival(s):
        return pltpu.make_async_remote_copy(
            src_ref=qbuf.at[s],
            dst_ref=qbuf.at[s],
            send_sem=q_send.at[s],
            recv_sem=q_recv.at[s],
            device_id={"sp": s},
            device_id_type=MESH,
        )

    for k in reversed(order):
        q_copy(peer(k)).start()

    for piece in (0, 1):

        @pl.when(blk < 2 - piece)
        def _():
            kv[pl.ds(piece * span, span), :] = jnp.zeros((span, 2 * HEAD), BF16)


    def own_shift(ref):
        row = ref[...].astype(F32).reshape(1, kv_heads * HEAD)
        mine = row[:, :HEAD]
        for h in range(1, kv_heads):
            mine = jnp.where(my_head == h, row[:, h * HEAD : (h + 1) * HEAD], mine)
        return mine

    key_shift = own_shift(kb_ref)
    value_shift = own_shift(vb_ref)

    relay = blks == 4

    def kv_copy(piece, dist, j):
        return pltpu.make_async_remote_copy(
            src_ref=kv.at[pl.ds(pl.multiple_of(piece * span + j * rows, rows), rows)],
            dst_ref=kv.at[pl.ds(pl.multiple_of((2 - dist) * span + j * rows, rows), rows)],
            send_sem=kv_send.at[dist - 1],
            recv_sem=kv_recv.at[dist - 1, j],
            device_id={"blk": lax.rem(blk + dist, blks)},
            device_id_type=MESH,
        )

    def kv_pass(j):
        kv_copy(2, 2, j).wait_recv()
        pltpu.make_async_remote_copy(
            src_ref=kv.at[pl.ds(pl.multiple_of(j * rows, rows), rows)],
            dst_ref=kv.at[pl.ds(pl.multiple_of(span + j * rows, rows), rows)],
            send_sem=kv_send.at[0],
            recv_sem=kv_recv.at[0, j],
            device_id={"blk": lax.rem(blk + blks - 1, blks)},
            device_id_type=MESH,
        ).start()

    near = blk + 1 < blks
    if relay:
        near = near & (blk != 1)
    sends = {1: near, 2: blk + 2 < blks}

    def finish(i, carry):
        j = place(i)
        at = rows_of(j)
        total = part_own[my_head, at, :]
        for k in range(1, pairs):
            s = lax.rem(my_pair + k, pairs)
            pltpu.make_async_remote_copy(
                src_ref=part_in.at[s, at],
                dst_ref=part_in.at[s, at],
                send_sem=part_send.at[s],
                recv_sem=part_recv.at[s, j],
                device_id={"sp": far(k)},
                device_id_type=MESH,
            ).wait_recv()
            total = total + part_in[s, at, :].astype(F32)
        keys = total[:, :HEAD] + key_shift
        turned = keys * cos_buf[at, :] + pltpu.roll(keys, HEAD // 2, 1) * sin_buf[at, :]
        put = pl.ds(pl.multiple_of(2 * span + j * rows, rows), rows)
        kv[put, :HEAD] = turned.astype(BF16)
        kv[put, HEAD:] = (total[:, HEAD:] + value_shift).astype(BF16)
        for dist in (2, 1):

            @pl.when(sends[dist])
            def _():
                kv_copy(2, dist, j).start()

        if relay:

            @pl.when((blk == 3) & (i >= 1))
            def _():
                kv_pass(place(i - 1))

        return carry

    lax.fori_loop(0, sp, finish, 0)
    if relay:

        @pl.when(blk == 3)
        def _():
            kv_pass(place(sp - 1))


    ends = []
    running = jnp.int32(0)
    for d in range(docs):
        running = running + docs_ref[d]
        ends.append(running)

    load_q.wait()
    for dist in (1, 2):

        arrives = blk >= dist
        if relay and dist == 2:
            arrives = arrives & (blk != 3)

        @pl.when(arrives)
        def _():
            for j in range(sp):
                kv_copy(2, dist, j).wait_recv()

    exponent = math.log2(math.e) / math.sqrt(HEAD)

    def attend(t):
        query_at = token_base + t * rows + lax.broadcasted_iota(jnp.int32, (rows, HEAD), 0)
        first = jnp.zeros((rows, HEAD), jnp.int32)
        for end in ends:
            first = jnp.where(query_at >= end, end, first)
        key_base = token_base - 2 * span + t * rows
        for c in range(window // HEAD):
            key_at = key_base + c * HEAD + lax.broadcasted_iota(jnp.int32, (rows, HEAD), 1)
            seen = (key_at >= first) & (key_at <= query_at)
            mask_buf[:, c * HEAD : (c + 1) * HEAD] = jnp.where(seen, 0.0, NEG_FILL)
        at = pl.ds(pl.multiple_of(t * rows, rows), window)
        for h in range(heads):
            cols = slice(h * HEAD, (h + 1) * HEAD)
            scores = lax.dot_general(
                qbuf[t, :, cols], kv[at, :HEAD], (((1,), (1,)), ((), ())), preferred_element_type=F32
            )
            scores = scores + mask_buf[...]
            largest = jnp.max(scores, axis=1, keepdims=True)
            weights = jnp.exp2((scores - largest) * exponent).astype(BF16)
            total = jnp.sum(weights.astype(F32), axis=1, keepdims=True)
            summed = jnp.dot(weights, kv[at, HEAD:], preferred_element_type=F32)
            obuf[t, :, cols] = (summed / total).astype(BF16)

    my_cols = pl.ds(pl.multiple_of(me * q_cols, q_cols), q_cols)

    def o_copy(d):
        return pltpu.make_async_remote_copy(
            src_ref=obuf.at[d],
            dst_ref=out_ref.at[0, :, my_cols],
            send_sem=o_send.at[d],
            recv_sem=o_recv.at[me],
            device_id={"sp": d},
            device_id_type=MESH,
        )

    def o_arrival(s):
        return pltpu.make_async_remote_copy(
            src_ref=obuf.at[s],
            dst_ref=out_ref.at[0, :, pl.ds(pl.multiple_of(s * q_cols, q_cols), q_cols)],
            send_sem=o_send.at[s],
            recv_sem=o_recv.at[s],
            device_id={"sp": s},
            device_id_type=MESH,
        )

    def each(k, carry):
        t = place(sp - k)
        q_arrival(t).wait_recv()
        attend(t)
        o_copy(t).start()
        return carry

    lax.fori_loop(1, sp, each, 0)
    attend(me)
    out_ref[0, :, my_cols] = obuf[me]

    for k in order:
        d = peer(k)
        o_arrival(d).wait_recv()
        o_copy(d).wait_send()
        feat_copy(k).wait_send()
        q_copy(d).wait_send()
        fwd_copy(d, feats.at[d, rep]).wait_send()
    fwd_copy(me, normed.at[me]).wait_send()

    def sent(sem, source):
        pltpu.make_async_remote_copy(
            src_ref=source,
            dst_ref=source,
            send_sem=sem,
            recv_sem=part_recv.at[0, 0],
            device_id={"sp": partner},
            device_id_type=MESH,
        ).wait_send()

    for slot in range(slots):
        sent(pair_send.at[slot], pair_in.at[slot])
    for k in range(1, pairs):
        sent(part_send.at[far(k) // 2], part_in.at[0])
    for dist in (1, 2):

        shipped = sends[dist]
        if relay and dist == 1:
            shipped = shipped | (blk == 3)

        @pl.when(shipped)
        def _():
            sent(kv_send.at[dist - 1], kv.at[pl.ds(0, span)])


def on_device(
    hidden,
    queries,
    norm_gain,
    key_matrix,
    value_matrix,
    key_shift_bias,
    value_shift_bias,
    doc_lengths,
):
    sp = lax.axis_size("sp")
    blks = lax.axis_size("blk")
    reps = lax.axis_size("rep")
    rows, width = hidden.shape[1:]
    half = rows // reps
    span = rows * sp
    fs = key_matrix.shape[0]
    kv_cols = key_matrix.shape[1]
    kv_heads = kv_cols // HEAD
    q_cols = queries.shape[2] // sp
    window = 2 * span + rows
    slots = kv_heads if sp > kv_heads else kv_heads // 2
    vmem = pl.BlockSpec(memory_space=pltpu.VMEM)
    anywhere = pl.BlockSpec(memory_space=pl.ANY)
    smem = pl.BlockSpec(memory_space=pltpu.SMEM)
    dma = pltpu.SemaphoreType.DMA
    return pl.pallas_call(
        functools.partial(kernel, (sp, blks, reps, rows)),
        out_shape=jax.ShapeDtypeStruct(queries.shape, BF16),
        in_specs=[anywhere, anywhere, vmem, anywhere, anywhere, vmem, vmem, smem],
        out_specs=vmem,
        scratch_shapes=[
            pltpu.VMEM((half, width), BF16),
            pltpu.VMEM((fs, 2 * kv_cols), BF16),
            pltpu.VMEM((sp, half, fs), BF16),
            pltpu.VMEM((sp, reps, half, fs), BF16),
            pltpu.VMEM((kv_heads, span, 2 * HEAD), F32),
            pltpu.VMEM((kv_heads, span, 2 * HEAD), BF16),
            pltpu.VMEM((slots, span, 2 * HEAD), BF16),
            pltpu.VMEM((slots, span, 2 * HEAD), BF16),
            pltpu.VMEM((sp // 2, span, 2 * HEAD), BF16),
            pltpu.VMEM((3 * span, 2 * HEAD), BF16),
            pltpu.VMEM((sp, rows, q_cols), BF16),
            pltpu.VMEM((sp, rows, q_cols), BF16),
            pltpu.VMEM((span, HEAD), F32),
            pltpu.VMEM((span, HEAD), F32),
            pltpu.VMEM((rows, window), F32),
            dma((4,)),
            dma((sp,)),
            dma((sp,)),
            dma((sp,)),
            dma((sp,)),
            dma((sp,)),
            dma((sp,)),
            dma((slots,)),
            dma((slots, sp)),
            dma((sp // 2,)),
            dma((sp // 2, sp)),
            dma((2,)),
            dma((2, sp)),
            dma((sp,)),
            dma((sp,)),
        ],
        compiler_params=pltpu.CompilerParams(
            collective_id=0, has_side_effects=True, vmem_limit_bytes=60 * 1024 * 1024
        ),
        name="masked_attention",
    )(
        hidden,
        queries,
        norm_gain.reshape(1, width),
        key_matrix,
        value_matrix,
        key_shift_bias,
        value_shift_bias,
        doc_lengths,
    )


def solution(mesh):
    in_specs = (
        P(("grp", "blk"), "sp", None),
        P(("grp", "blk"), "sp", "rep"),
        P(),
        P("sp", "rep"),
        P("sp", "rep"),
        P("rep"),
        P("rep"),
        P("grp"),
    )
    out_specs = P(("grp", "blk"), "sp", "rep")
    return jax.shard_map(
        on_device, mesh=mesh, in_specs=in_specs, out_specs=out_specs, check_vma=False
    )
```

profile of v0, /device:TPU:0, one launch (start us, length us, event | category | flops | bytes accessed | tf_op | source)
XLA Modules:
  0.0 65.8 jit_solution(16545572000999769663)
XLA Ops:
  0.0 63.9 %masked_attention.1 = bf16[1,128,2048]{2,1,0:T(8,128)(2,1)} custom-call(bf16[1,128,4096]{2,1,0:T(8,128)(2,1)} %hidden_ref.1, bf16[1,128,2048]{2,1,0:T(8,128)(2,1)} %queries_ref.1, f32[1,4096]{1,0:T(1,128)} %bitcast.1, bf16[1024,512]{1,0:T(8,128)(2,1)} %kw_ref.1, bf16[1024,512]{1,0:T(8,128)(2,1)} %vw_ref.1, bf16[512]{0:T(512)(128)(2,1)} %kb_ref.1, ...), custom_call_target="tpu_custom_call" | custom-call | tf_op jit(solution)/shard_map/masked_attention/pallas_call | solution.py:509
  63.9 1.9 %copy.10 = bf16[1,128,2048]{2,1,0:T(8,128)(2,1)} copy(bf16[1,128,2048]{2,1,0:T(8,128)(2,1)} %masked_attention.1) | data formatting | bytes 1048576
where the time goes:
time: 66.8 us; the launch traced here: 65.8 us
  Pallas kernels  63.9 us (96%)
  local copies, waits for them, and re-layouts  1.88 us (3%)
    pallas_call x1, Pallas kernels, on_device(): pl.pallas_call(functools.partial(kernel, (sp, blks, reps, rows)), out_sha...  63.9 us
    unnamed x1, local copies, waits for them, and re-layouts  1.88 us

commit v1 on v0

--- a/solution.py
+++ b/solution.py
@@ -480,6 +480,598 @@
             sent(kv_send.at[dist - 1], kv.at[pl.ds(0, span)])
 
 
+def heads_kernel(
+    sizes,
+    hidden_ref,
+    queries_ref,
+    gain_ref,
+    kw_ref,
+    vw_ref,
+    kb_ref,
+    vb_ref,
+    docs_ref,
+    out_ref,
+    hid,
+    wts,
+    normed,
+    feats,
+    own,
+    up_in,
+    up_out,
+    down_in,
+    down_out,
+    self_out,
+    self_in,
+    up_last,
+    down_last,
+    kv,
+    qbuf,
+    obuf,
+    total,
+    cos_buf,
+    sin_buf,
+    mask_buf,
+    load_sem,
+    feat_send,
+    feat_recv,
+    fwd_send,
+    fwd_recv,
+    q_send,
+    q_recv,
+    self_send,
+    self_recv,
+    up_send,
+    up_recv,
+    up_last_send,
+    up_last_recv,
+    down_send,
+    down_recv,
+    down_last_send,
+    down_last_recv,
+    rise_send,
+    rise_recv,
+    fall_send,
+    fall_recv,
+    o_send,
+    o_recv,
+):
+    sp, blks, reps, rows, chunks = sizes
+    me = lax.axis_index("sp")
+    blk = lax.axis_index("blk")
+    rep = lax.axis_index("rep")
+    span = sp * rows
+    cut = rows // chunks
+    part = cut // reps
+    fs = kw_ref.shape[0]
+    q_cols = queries_ref.shape[2] // blks
+    heads = q_cols // HEAD
+    docs = docs_ref.shape[0]
+    window = 2 * span + rows
+    last = sp - 1
+    pair = 2 * HEAD
+
+    def group(k):
+        return lax.rem(blk + k, blks)
+
+    barrier = pltpu.get_barrier_semaphore()
+    for k in range(1, sp):
+        pl.semaphore_signal(
+            barrier, inc=1, device_id={"sp": lax.rem(me + k, sp)}, device_id_type=MESH
+        )
+    for k in range(1, reps):
+        pl.semaphore_signal(
+            barrier, inc=1, device_id={"rep": lax.rem(rep + k, reps)}, device_id_type=MESH
+        )
+    for k in range(1, blks):
+        pl.semaphore_signal(barrier, inc=1, device_id={"blk": group(k)}, device_id_type=MESH)
+
+        @pl.when(me > 0)
+        def _():
+            pl.semaphore_signal(
+                barrier, inc=1, device_id={"sp": me - 1, "blk": group(k)}, device_id_type=MESH
+            )
+
+        @pl.when(me < last)
+        def _():
+            pl.semaphore_signal(
+                barrier, inc=1, device_id={"sp": me + 1, "blk": group(k)}, device_id_type=MESH
+            )
+
+    def load_hid(q):
+        return pltpu.make_async_copy(
+            hidden_ref.at[0, pl.ds(pl.multiple_of(q * cut + rep * part, part), part)],
+            hid.at[q],
+            load_sem.at[q],
+        )
+
+    def load_w(g, side):
+        source = vw_ref if side else kw_ref
+        return pltpu.make_async_copy(
+            source.at[:, g * HEAD : (g + 1) * HEAD],
+            wts.at[:, (2 * g + side) * HEAD : (2 * g + side + 1) * HEAD],
+            load_sem.at[chunks + 2 * g + side],
+        )
+
+    own_cols = pl.ds(pl.multiple_of(blk * q_cols, q_cols), q_cols)
+    load_q = pltpu.make_async_copy(
+        queries_ref.at[0, :, own_cols], qbuf.at[blk], load_sem.at[chunks + 2 * blks]
+    )
+    for q in range(chunks):
+        load_hid(q).start()
+    for g in range(blks):
+        load_w(g, 0).start()
+        load_w(g, 1).start()
+    load_q.start()
+
+    def feat_copy(q, d):
+        return pltpu.make_async_remote_copy(
+            src_ref=normed.at[q, d],
+            dst_ref=feats.at[q, me, rep],
+            send_sem=feat_send,
+            recv_sem=feat_recv.at[q, me],
+            device_id={"sp": d},
+            device_id_type=MESH,
+        )
+
+    def feat_arrival(q, s):
+        return pltpu.make_async_remote_copy(
+            src_ref=normed.at[q, 0],
+            dst_ref=feats.at[q, s, rep],
+            send_sem=feat_send,
+            recv_sem=feat_recv.at[q, s],
+            device_id={"sp": s},
+            device_id_type=MESH,
+        )
+
+    other = lax.rem(rep + 1, reps)
+
+    def fwd_copy(q, s, source):
+        return pltpu.make_async_remote_copy(
+            src_ref=source,
+            dst_ref=feats.at[q, s, rep],
+            send_sem=fwd_send,
+            recv_sem=fwd_recv.at[q],
+            device_id={"rep": other},
+            device_id_type=MESH,
+        )
+
+    def q_copy(g):
+        return pltpu.make_async_remote_copy(
+            src_ref=queries_ref.at[0, :, pl.ds(pl.multiple_of(g * q_cols, q_cols), q_cols)],
+            dst_ref=qbuf.at[blk],
+            send_sem=q_send,
+            recv_sem=q_recv,
+            device_id={"blk": g},
+            device_id_type=MESH,
+        )
+
+    def norm(q):
+        load_hid(q).wait()
+        values = hid[q].astype(F32)
+        scale = lax.rsqrt(jnp.mean(values * values, axis=1, keepdims=True) + EPS_VALUE)
+        for d in range(sp):
+            cols = slice(d * fs, (d + 1) * fs)
+            normed[q, d] = (hid[q, :, cols].astype(F32) * scale * gain_ref[:, cols]).astype(BF16)
+
+    for q in range(chunks):
+        norm(q)
+    peers = sp - 1 + reps - 1 + blks - 1
+
+    @pl.when((me == 0) | (me == last))
+    def _():
+        pl.semaphore_wait(barrier, peers + blks - 1)
+
+    @pl.when((me > 0) & (me < last))
+    def _():
+        pl.semaphore_wait(barrier, peers + 2 * (blks - 1))
+
+    for q in range(chunks):
+        for step in range(1, sp):
+            far = jnp.where(rep == 0, step, sp - step)
+
+            @pl.when(me + far < sp)
+            def _():
+                feat_copy(q, me + far).start()
+
+            @pl.when(me >= far)
+            def _():
+                feat_copy(q, me - far).start()
+
+        fwd_copy(q, me, normed.at[q, me]).start()
+        feats[q, me, rep] = normed[q, me]
+    for k in range(1, blks):
+        q_copy(group(k)).start()
+
+    lanes = lax.broadcasted_iota(jnp.int32, (1, HEAD), 1)
+    index = lax.rem(lanes, HEAD // 2).astype(F32)
+    inverse = jnp.exp(index * (-2.0 * math.log(THETA_BASE) / HEAD))
+    sign = jnp.where(lanes < HEAD // 2, -1.0, 1.0)
+
+    def angle_step(c, carry):
+        places = c * span + me * rows + lax.broadcasted_iota(jnp.int32, (rows, HEAD), 0)
+        angles = places.astype(F32) * inverse
+        cos_buf[c] = jnp.cos(angles)
+        sin_buf[c] = jnp.sin(angles) * sign
+        return carry
+
+    lax.fori_loop(0, blks, angle_step, 0)
+    kv[: 2 * span, :pair] = jnp.zeros((2 * span, pair), BF16)
+    kv[:, pair:] = jnp.ones((kv.shape[0], HEAD), BF16)
+
+    def own_shift(ref):
+        row = ref[...].astype(F32).reshape(1, blks * HEAD)
+        mine = row[:, :HEAD]
+        for g in range(1, blks):
+            mine = jnp.where(blk == g, row[:, g * HEAD : (g + 1) * HEAD], mine)
+        return mine
+
+    key_shift = own_shift(kb_ref)
+    value_shift = own_shift(vb_ref)
+
+    def landed(sem, ref):
+        pltpu.make_async_remote_copy(
+            src_ref=ref,
+            dst_ref=ref,
+            send_sem=sem,
+            recv_sem=sem,
+            device_id={"rep": other},
+            device_id_type=MESH,
+        ).wait_recv()
+
+    def left(sem, ref):
+        pltpu.make_async_remote_copy(
+            src_ref=ref,
+            dst_ref=ref,
+            send_sem=sem,
+            recv_sem=sem,
+            device_id={"rep": other},
+            device_id_type=MESH,
+        ).wait_send()
+
+    def self_copy(q, g):
+        return pltpu.make_async_remote_copy(
+            src_ref=self_out.at[q, g],
+            dst_ref=self_in.at[q, blk],
+            send_sem=self_send,
+            recv_sem=self_recv.at[q],
+            device_id={"blk": g},
+            device_id_type=MESH,
+        )
+
+    def project(q):
+        for far in range(1, sp):
+
+            @pl.when(me >= far)
+            def _():
+                feat_arrival(q, me - far).wait_recv()
+                fwd_copy(q, me - far, feats.at[q, me - far, rep]).start()
+
+            @pl.when(me + far < sp)
+            def _():
+                feat_arrival(q, me + far).wait_recv()
+                fwd_copy(q, me + far, feats.at[q, me + far, rep]).start()
+
+        landed(fwd_recv.at[q], normed.at[q])
+        partial = jnp.dot(
+            feats[q].reshape(sp * cut, fs), wts[...], preferred_element_type=F32
+        )
+        for j in range(sp):
+            for g in range(blks):
+                own[q, j, g] = partial[j * cut : (j + 1) * cut, g * pair : (g + 1) * pair]
+
+    def keep(q):
+        for k in range(1, blks):
+            g = group(k)
+            self_out[q, g] = own[q, me, g].astype(BF16)
+            self_copy(q, g).start()
+        self_in[q, blk] = own[q, me, blk].astype(BF16)
+
+    def hop(q, t, d, up):
+        to = t + 1 if up else t - 1
+        came = t > 0 if up else t < last
+        inbound, outbound = (up_in, up_out) if up else (down_in, down_out)
+        sent, arrived = (up_send, up_recv) if up else (down_send, down_recv)
+        lands = up_last if up else down_last
+        land_sent, landed_sem = (up_last_send, up_last_recv) if up else (down_last_send, down_last_recv)
+        if came:
+            landed(arrived.at[q, d], inbound.at[q, d])
+        for g in range(blks):
+            value = own[q, d, g]
+            if came:
+                value = value + inbound[q, d, g].astype(F32)
+            outbound[q, d, g] = value.astype(BF16)
+        if d != to:
+            pltpu.make_async_remote_copy(
+                src_ref=outbound.at[q, d],
+                dst_ref=inbound.at[q, d],
+                send_sem=sent,
+                recv_sem=arrived.at[q, d],
+                device_id={"sp": to},
+                device_id_type=MESH,
+            ).start()
+        else:
+            for k in range(blks):
+                g = group(k)
+                pltpu.make_async_remote_copy(
+                    src_ref=outbound.at[q, d, g],
+                    dst_ref=lands.at[q, blk],
+                    send_sem=land_sent,
+                    recv_sem=landed_sem.at[q],
+                    device_id={"sp": to, "blk": g},
+                    device_id_type=MESH,
+                ).start()
+
+    def relay(q, t, d):
+        @pl.when(me == t)
+        def _():
+            hop(q, t, d, True)
+
+        @pl.when(me == last - t)
+        def _():
+            hop(q, last - t, last - d, False)
+
+    def place(q, c, j):
+        return pl.ds(pl.multiple_of(2 * span + (c * sp + j) * rows + q * cut, cut), cut)
+
+    sent_cols = slice(0, pair)
+
+    def rise(q, j):
+        for c in range(blks):
+            pltpu.make_async_remote_copy(
+                src_ref=kv.at[place(q, c, j), sent_cols],
+                dst_ref=kv.at[place(q, c, j), sent_cols],
+                send_sem=rise_send,
+                recv_sem=rise_recv.at[q, j],
+                device_id={"sp": me + 1},
+                device_id_type=MESH,
+            ).start()
+
+    def fall(q, j):
+        for c in range(blks):
+            pltpu.make_async_remote_copy(
+                src_ref=kv.at[place(q, c, j), sent_cols],
+                dst_ref=kv.at[place(q, c, j), sent_cols],
+                send_sem=fall_send,
+                recv_sem=fall_recv.at[q, j],
+                device_id={"sp": me - 1},
+                device_id_type=MESH,
+            ).start()
+
+    def close(q):
+        landed(self_recv.at[q], self_in.at[q, pl.ds(0, blks - 1)])
+        total[...] = self_in[q].astype(F32)
+
+        @pl.when(me > 0)
+        def _():
+            landed(up_last_recv.at[q], up_last.at[q])
+            total[...] = total[...] + up_last[q].astype(F32)
+
+        @pl.when(me < last)
+        def _():
+            landed(down_last_recv.at[q], down_last.at[q])
+            total[...] = total[...] + down_last[q].astype(F32)
+
+        at = slice(q * cut, (q + 1) * cut)
+        for c in range(blks):
+            keys = total[c, :, :HEAD] + key_shift
+            turned = keys * cos_buf[c, at] + pltpu.roll(keys, HEAD // 2, 1) * sin_buf[c, at]
+            kv[place(q, c, me), :HEAD] = turned.astype(BF16)
+            kv[place(q, c, me), HEAD:pair] = (total[c, :, HEAD:] + value_shift).astype(BF16)
+
+        @pl.when(me < last)
+        def _():
+            rise(q, me)
+
+        @pl.when(me > 0)
+        def _():
+            fall(q, me)
+
+    every = kv.at[pl.ds(0, blks * cut), sent_cols]
+
+    def gather(q, t, j):
+        @pl.when(me == t)
+        def _():
+            landed(rise_recv.at[q, j], every)
+            if t < last:
+                rise(q, j)
+
+        @pl.when(me == last - t)
+        def _():
+            landed(fall_recv.at[q, last - j], every)
+            if t < last:
+                fall(q, last - j)
+
+    ends = []
+    running = jnp.int32(0)
+    for d in range(docs):
+        running = running + docs_ref[d]
+        ends.append(running)
+
+    exponent = math.log2(math.e) / math.sqrt(HEAD)
+
+    def attend(c):
+        query_at = c * span + me * rows + lax.broadcasted_iota(jnp.int32, (rows, HEAD), 0)
+        first = jnp.zeros((rows, HEAD), jnp.int32)
+        for end in ends:
+            first = jnp.where(query_at >= end, end, first)
+        base = c * span + me * rows - 2 * span
+        for piece in range(window // HEAD):
+            key_at = base + piece * HEAD + lax.broadcasted_iota(jnp.int32, (rows, HEAD), 1)
+            seen = (key_at >= first) & (key_at <= query_at)
+            mask_buf[:, piece * HEAD : (piece + 1) * HEAD] = jnp.where(seen, 0.0, NEG_FILL)
+        at = pl.ds(pl.multiple_of(c * span + me * rows, rows), window)
+        for h in range(heads):
+            cols = slice(h * HEAD, (h + 1) * HEAD)
+            scores = lax.dot_general(
+                qbuf[c, :, cols], kv[at, :HEAD], (((1,), (1,)), ((), ())), preferred_element_type=F32
+            )
+            scores = scores + mask_buf[...]
+            largest = jnp.max(scores, axis=1, keepdims=True)
+            weights = jnp.exp2((scores - largest) * exponent).astype(BF16)
+            summed = jnp.dot(weights, kv[at, HEAD:], preferred_element_type=F32)
+            obuf[c, :, cols] = (summed[:, :HEAD] / summed[:, HEAD:]).astype(BF16)
+
+    def o_copy(c):
+        return pltpu.make_async_remote_copy(
+            src_ref=obuf.at[c],
+            dst_ref=out_ref.at[0, :, own_cols],
+            send_sem=o_send,
+            recv_sem=o_recv,
+            device_id={"blk": c},
+            device_id_type=MESH,
+        )
+
+    def weights_in():
+        for g in range(blks):
+            load_w(g, 0).wait()
+            load_w(g, 1).wait()
+
+    def queries_in():
+        load_q.wait()
+        landed(q_recv, qbuf.at[pl.ds(0, blks - 1)])
+
+    def finish(k, carry):
+        c = group(k)
+        attend(c)
+        o_copy(c).start()
+        return carry
+
+    period, lag, start = 16.8 / chunks, 1.0, 12.0
+    unit = period / last
+    events = []
+    for q in range(chunks):
+        begin = start + period * q
+
+        def first_step(q=q):
+            if q == 0:
+                weights_in()
+            project(q)
+            for d in range(last, 0, -1):
+                relay(q, 0, d)
+            keep(q)
+
+        events.append((5.4 + 11.2 / chunks * (q + 1), first_step, ()))
+        for t in range(1, last):
+            for d in range(last, t, -1):
+                arrival = begin + unit * (last - d + 1) + (t - 1) * (unit + lag) + lag
+                events.append((arrival, relay, (q, t, d)))
+        closed = begin + unit + (last - 1) * (unit + lag) + lag
+        events.append((closed, close, (q,)))
+        for j in range(last):
+            free = closed
+            if j == 0:
+                free = max(closed, start + period * chunks + unit * q)
+            for t in range(j + 1, sp):
+                events.append((free + (t - j) * (unit + lag), gather, (q, t, j)))
+    events.sort(key=lambda e: e[0])
+    for _, step, taken in events:
+        step(*taken)
+    queries_in()
+
+    lax.fori_loop(1, blks, finish, 0)
+    attend(blk)
+    out_ref[0, :, own_cols] = obuf[blk]
+
+    some = pl.ds(0, blks - 1)
+    left(feat_send, normed.at[:, pl.ds(0, sp - 1)])
+    left(fwd_send, normed)
+    left(self_send, self_out.at[:, some])
+    left(q_send, qbuf.at[some])
+    for t in range(sp):
+
+        @pl.when(me == t)
+        def _():
+            if t < last - 1:
+                left(up_send, up_out.at[:, pl.ds(0, last - t - 1)])
+            if t > 1:
+                left(down_send, down_out.at[:, pl.ds(0, t - 1)])
+            if t < last:
+                left(up_last_send, up_last)
+                left(rise_send, kv.at[pl.ds(0, blks * rows * (t + 1)), sent_cols])
+            if t > 0:
+                left(down_last_send, down_last)
+                left(fall_send, kv.at[pl.ds(0, blks * rows * (sp - t)), sent_cols])
+
+    landed(o_recv, obuf.at[some])
+    left(o_send, obuf.at[some])
+
+
+CHUNKS = 4
+
+
+def heads_call(operands, sp, blks, reps):
+    hidden, queries, _, key_matrix = operands[:4]
+    rows, width = hidden.shape[1:]
+    chunks = CHUNKS
+    cut = rows // chunks
+    span = rows * sp
+    fs, kv_cols = key_matrix.shape
+    q_cols = queries.shape[2] // blks
+    pair = 2 * HEAD
+    vmem = pl.BlockSpec(memory_space=pltpu.VMEM)
+    anywhere = pl.BlockSpec(memory_space=pl.ANY)
+    smem = pl.BlockSpec(memory_space=pltpu.SMEM)
+    dma = pltpu.SemaphoreType.DMA
+    by_sp, each = dma((chunks, sp)), dma((chunks,))
+    line = pltpu.VMEM((chunks, sp, blks, cut, pair), BF16)
+    spot = pltpu.VMEM((chunks, blks, cut, pair), BF16)
+    return pl.pallas_call(
+        functools.partial(heads_kernel, (sp, blks, reps, rows, chunks)),
+        out_shape=jax.ShapeDtypeStruct(queries.shape, BF16),
+        in_specs=[anywhere, anywhere, vmem, anywhere, anywhere, vmem, vmem, smem],
+        out_specs=vmem,
+        scratch_shapes=[
+            pltpu.VMEM((chunks, cut // reps, width), BF16),
+            pltpu.VMEM((fs, 2 * kv_cols), BF16),
+            pltpu.VMEM((chunks, sp, cut // reps, fs), BF16),
+            pltpu.VMEM((chunks, sp, reps, cut // reps, fs), BF16),
+            pltpu.VMEM((chunks, sp, blks, cut, pair), F32),
+            line,
+            line,
+            line,
+            line,
+            spot,
+            spot,
+            spot,
+            spot,
+            pltpu.VMEM(((2 + blks) * span, 3 * HEAD), BF16),
+            pltpu.VMEM((blks, rows, q_cols), BF16),
+            pltpu.VMEM((blks, rows, q_cols), BF16),
+            pltpu.VMEM((blks, cut, pair), F32),
+            pltpu.VMEM((blks, rows, HEAD), F32),
+            pltpu.VMEM((blks, rows, HEAD), F32),
+            pltpu.VMEM((rows, 2 * span + rows), F32),
+            dma((chunks + 2 * blks + 1,)),
+            dma,
+            by_sp,
+            dma,
+            each,
+            dma,
+            dma,
+            dma,
+            each,
+            dma,
+            by_sp,
+            dma,
+            each,
+            dma,
+            by_sp,
+            dma,
+            each,
+            dma,
+            by_sp,
+            dma,
+            by_sp,
+            dma,
+            dma,
+        ],
+        compiler_params=pltpu.CompilerParams(
+            collective_id=0, has_side_effects=True, vmem_limit_bytes=60 * 1024 * 1024
+        ),
+        name="masked_attention",
+    )(*operands)
+
+
 def on_device(
     hidden,
     queries,
@@ -502,6 +1094,18 @@
     q_cols = queries.shape[2] // sp
     window = 2 * span + rows
     slots = kv_heads if sp > kv_heads else kv_heads // 2
+    operands = (
+        hidden,
+        queries,
+        norm_gain.reshape(1, width),
+        key_matrix,
+        value_matrix,
+        key_shift_bias,
+        value_shift_bias,
+        doc_lengths,
+    )
+    if blks == kv_heads:
+        return heads_call(operands, sp, blks, reps)
     vmem = pl.BlockSpec(memory_space=pltpu.VMEM)
     anywhere = pl.BlockSpec(memory_space=pl.ANY)
     smem = pl.BlockSpec(memory_space=pltpu.SMEM)
@@ -547,16 +1151,7 @@
             collective_id=0, has_side_effects=True, vmem_limit_bytes=60 * 1024 * 1024
         ),
         name="masked_attention",
-    )(
-        hidden,
-        queries,
-        norm_gain.reshape(1, width),
-        key_matrix,
-        value_matrix,
-        key_shift_bias,
-        value_shift_bias,
-        doc_lengths,
-    )
+    )(*operands)
 
 
 def solution(mesh):

time: 66.8 us -> 64.6 us (0.967); the launches traced: 65.8 us -> 64.4 us
  Pallas kernels: 63.9 us -> 62.5 us
    pallas_call x1, Pallas kernels: 63.9 us -> 62.5 us  [heads_call(): pl.pallas_call(functools.partial(heads_kernel, (sp, blks, reps, rows, chu...]
where the time goes in v1:
time: 64.6 us; the launch traced here: 64.4 us
  Pallas kernels  62.5 us (97%)
  local copies, waits for them, and re-layouts  1.88 us (3%)
    pallas_call x1, Pallas kernels, heads_call(): pl.pallas_call(functools.partial(heads_kernel, (sp, blks, reps, rows, chu...  62.5 us
    unnamed x1, local copies, waits for them, and re-layouts  1.88 us

profile of v1, /device:TPU:0, one launch (start us, length us, event | category | flops | bytes accessed | tf_op | source)
XLA Modules:
  0.0 64.4 jit_solution(16045276327354681706)
XLA Ops:
  0.0 62.5 %masked_attention.1 = bf16[1,128,2048]{2,1,0:T(8,128)(2,1)} custom-call(bf16[1,128,4096]{2,1,0:T(8,128)(2,1)} %hidden_ref.1, bf16[1,128,2048]{2,1,0:T(8,128)(2,1)} %queries_ref.1, f32[1,4096]{1,0:T(1,128)} %bitcast.1, bf16[1024,512]{1,0:T(8,128)(2,1)} %kw_ref.1, bf16[1024,512]{1,0:T(8,128)(2,1)} %vw_ref.1, bf16[512]{0:T(512)(128)(2,1)} %kb_ref.1, ...), custom_call_target="tpu_custom_call" | custom-call | tf_op jit(solution)/shard_map/masked_attention/pallas_call | solution.py:1018
  62.5 1.9 %copy.10 = bf16[1,128,2048]{2,1,0:T(8,128)(2,1)} copy(bf16[1,128,2048]{2,1,0:T(8,128)(2,1)} %masked_attention.1) | data formatting | bytes 1048576

commit v2 on v1

--- a/solution.py
+++ b/solution.py
@@ -550,8 +550,10 @@
     last = sp - 1
     pair = 2 * HEAD
 
+    turn = 2 * lax.rem(blk, 2) - 1
+
     def group(k):
-        return lax.rem(blk + k, blks)
+        return lax.rem(blk + blks + k * turn, blks)
 
     barrier = pltpu.get_barrier_semaphore()
     for k in range(1, sp):
@@ -653,8 +655,7 @@
             cols = slice(d * fs, (d + 1) * fs)
             normed[q, d] = (hid[q, :, cols].astype(F32) * scale * gain_ref[:, cols]).astype(BF16)
 
-    for q in range(chunks):
-        norm(q)
+    norm(0)
     peers = sp - 1 + reps - 1 + blks - 1
 
     @pl.when((me == 0) | (me == last))
@@ -666,6 +667,8 @@
         pl.semaphore_wait(barrier, peers + 2 * (blks - 1))
 
     for q in range(chunks):
+        if q > 0:
+            norm(q)
         for step in range(1, sp):
             far = jnp.where(rep == 0, step, sp - step)
 
@@ -866,6 +869,16 @@
         def _():
             fall(q, me)
 
+    def close_inner(q):
+        @pl.when((me > 0) & (me < last))
+        def _():
+            close(q)
+
+    def close_outer(q):
+        @pl.when((me == 0) | (me == last))
+        def _():
+            close(q)
+
     every = kv.at[pl.ds(0, blks * cut), sent_cols]
 
     def gather(q, t, j):
@@ -931,38 +944,53 @@
         landed(q_recv, qbuf.at[pl.ds(0, blks - 1)])
 
     def finish(k, carry):
-        c = group(k)
-        attend(c)
-        o_copy(c).start()
+        attend(group(k))
+        o_copy(group(k)).start()
         return carry
 
-    period, lag, start = 16.8 / chunks, 1.0, 12.0
-    unit = period / last
+    unit, hop_time, lead = 5.6 / chunks, 3.3, 12.0
+    inner_late, outer_late, gather_late, first_late = 1.0, 0.0, 1.5, 0.0
+    hold = 0
+    feed_first, feed_step = 10.0, 11.2 / chunks
+    queue = []
+    for q in range(chunks + hold):
+        if q < chunks:
+            queue.append((q, last))
+        if q >= hold and hold:
+            queue.append((q - hold, 1))
+        if q < chunks:
+            queue.extend((q, d) for d in range(last - 1, 0 if not hold else 1, -1))
+    came = {item: lead + unit * (n + 1) + 1.0 for n, item in enumerate(queue)}
+    fed = lead + unit * len(queue) + 1.0
     events = []
     for q in range(chunks):
-        begin = start + period * q
 
         def first_step(q=q):
             if q == 0:
                 weights_in()
             project(q)
-            for d in range(last, 0, -1):
-                relay(q, 0, d)
+            begin = queue.index((q, last))
+            end = queue.index((q + 1, last)) if q + 1 < chunks else len(queue)
+            for n in range(begin, end):
+                relay(queue[n][0], 0, queue[n][1])
             keep(q)
 
-        events.append((5.4 + 11.2 / chunks * (q + 1), first_step, ()))
+        events.append((feed_first + feed_step * q, first_step, ()))
         for t in range(1, last):
             for d in range(last, t, -1):
-                arrival = begin + unit * (last - d + 1) + (t - 1) * (unit + lag) + lag
-                events.append((arrival, relay, (q, t, d)))
-        closed = begin + unit + (last - 1) * (unit + lag) + lag
-        events.append((closed, close, (q,)))
+                events.append((came[q, d] + hop_time * (t - 1), relay, (q, t, d)))
+        inner = max(came[q, 1], came[q, last - 1] + hop_time) + inner_late
+        outer = came[q, last] + hop_time * (last - 1) + outer_late
+        events.append((inner, close_inner, (q,)))
+        events.append((outer, close_outer, (q,)))
         for j in range(last):
-            free = closed
-            if j == 0:
-                free = max(closed, start + period * chunks + unit * q)
             for t in range(j + 1, sp):
-                events.append((free + (t - j) * (unit + lag), gather, (q, t, j)))
+                if j == 0:
+                    come = max(outer + hop_time, fed + unit * (q + 1)) + first_late
+                else:
+                    come = inner + hop_time + gather_late
+                when = come + (t - j - 1) * hop_time
+                events.append((1000.0 + when if t == last else when, gather, (q, t, j)))
     events.sort(key=lambda e: e[0])
     for _, step, taken in events:
         step(*taken)
@@ -1017,7 +1045,7 @@
     spot = pltpu.VMEM((chunks, blks, cut, pair), BF16)
     return pl.pallas_call(
         functools.partial(heads_kernel, (sp, blks, reps, rows, chunks)),
-        out_shape=jax.ShapeDtypeStruct(queries.shape, BF16),
+        out_shape=pltpu.VMEM(queries.shape, BF16),
         in_specs=[anywhere, anywhere, vmem, anywhere, anywhere, vmem, vmem, smem],
         out_specs=vmem,
         scratch_shapes=[

time: 64.6 us -> 60 us (0.929)
  Pallas kernels: 62.5 us -> 59 us
  local copies, waits for them, and re-layouts: 1.88 us -> 0.8 us
    pallas_call x1, Pallas kernels: 62.5 us -> 59 us  [heads_call(): pl.pallas_call(functools.partial(heads_kernel, (sp, blks, reps, rows, chu...]
    unnamed x1, local copies, waits for them, and re-layouts: 1.88 us -> 0.8 us
where the time goes in v2:
time: 60 us; the launch traced here: 59.8 us
  Pallas kernels  59 us (98%)
  local copies, waits for them, and re-layouts  0.8 us (1%)
    pallas_call x1, Pallas kernels, heads_call(): pl.pallas_call(functools.partial(heads_kernel, (sp, blks, reps, rows, chu...  59 us

profile of v2, /device:TPU:0, one launch (start us, length us, event | category | flops | bytes accessed | tf_op | source)
XLA Modules:
  0.0 59.8 jit_solution(17693867772925411951)
XLA Ops:
  0.0 59.0 %masked_attention.1 = bf16[1,128,2048]{2,1,0:T(8,128)(2,1)S(1)} custom-call(bf16[1,128,4096]{2,1,0:T(8,128)(2,1)} %hidden_ref.1, bf16[1,128,2048]{2,1,0:T(8,128)(2,1)} %queries_ref.1, f32[1,4096]{1,0:T(1,128)} %bitcast.1, bf16[1024,512]{1,0:T(8,128)(2,1)} %kw_ref.1, bf16[1024,512]{1,0:T(8,128)(2,1)} %vw_ref.1, bf16[512]{0:T(512)(128)(2,1)} %kb_ref.1, ...), custom_call_target="tpu_custom_call" | custom-call | tf_op jit(solution)/shard_map/masked_attention/pallas_call | solution.py:1046
  59.0 0.8 %copy.10 = bf16[1,128,2048]{2,1,0:T(8,128)(2,1)} copy(bf16[1,128,2048]{2,1,0:T(8,128)(2,1)S(1)} %masked_attention.1) | data formatting | bytes 1048576

commit v3 on v2

--- a/solution.py
+++ b/solution.py
@@ -830,7 +830,7 @@
             ).start()
 
     def fall(q, j):
-        for c in range(blks):
+        for c in range(blks - 1):
             pltpu.make_async_remote_copy(
                 src_ref=kv.at[place(q, c, j), sent_cols],
                 dst_ref=kv.at[place(q, c, j), sent_cols],
@@ -880,6 +880,7 @@
             close(q)
 
     every = kv.at[pl.ds(0, blks * cut), sent_cols]
+    fallen = kv.at[pl.ds(0, (blks - 1) * cut), sent_cols]
 
     def gather(q, t, j):
         @pl.when(me == t)
@@ -890,7 +891,7 @@
 
         @pl.when(me == last - t)
         def _():
-            landed(fall_recv.at[q, last - j], every)
+            landed(fall_recv.at[q, last - j], fallen)
             if t < last:
                 fall(q, last - j)
 
@@ -902,7 +903,7 @@
 
     exponent = math.log2(math.e) / math.sqrt(HEAD)
 
-    def attend(c):
+    def mask_step(c, carry):
         query_at = c * span + me * rows + lax.broadcasted_iota(jnp.int32, (rows, HEAD), 0)
         first = jnp.zeros((rows, HEAD), jnp.int32)
         for end in ends:
@@ -911,18 +912,25 @@
         for piece in range(window // HEAD):
             key_at = base + piece * HEAD + lax.broadcasted_iota(jnp.int32, (rows, HEAD), 1)
             seen = (key_at >= first) & (key_at <= query_at)
-            mask_buf[:, piece * HEAD : (piece + 1) * HEAD] = jnp.where(seen, 0.0, NEG_FILL)
+            mask_buf[c, :, piece * HEAD : (piece + 1) * HEAD] = jnp.where(seen, 0.0, NEG_FILL)
+        return carry
+
+    def attend(c):
         at = pl.ds(pl.multiple_of(c * span + me * rows, rows), window)
-        for h in range(heads):
-            cols = slice(h * HEAD, (h + 1) * HEAD)
+        for h in range(0, heads, 2):
+            parts = [slice(n * HEAD, (n + 1) * HEAD) for n in range(h, min(h + 2, heads))]
+            stacked = jnp.concatenate([qbuf[c, :, cols] for cols in parts], axis=0)
             scores = lax.dot_general(
-                qbuf[c, :, cols], kv[at, :HEAD], (((1,), (1,)), ((), ())), preferred_element_type=F32
+                stacked, kv[at, :HEAD], (((1,), (1,)), ((), ())), preferred_element_type=F32
             )
-            scores = scores + mask_buf[...]
+            scores = scores.reshape(len(parts), rows, window) + mask_buf[c][None]
+            scores = scores.reshape(len(parts) * rows, window)
             largest = jnp.max(scores, axis=1, keepdims=True)
             weights = jnp.exp2((scores - largest) * exponent).astype(BF16)
             summed = jnp.dot(weights, kv[at, HEAD:], preferred_element_type=F32)
-            obuf[c, :, cols] = (summed[:, :HEAD] / summed[:, HEAD:]).astype(BF16)
+            result = (summed[:, :HEAD] / summed[:, HEAD:]).astype(BF16)
+            for n, cols in enumerate(parts):
+                obuf[c, :, cols] = result[n * rows : (n + 1) * rows]
 
     def o_copy(c):
         return pltpu.make_async_remote_copy(
@@ -948,7 +956,7 @@
         o_copy(group(k)).start()
         return carry
 
-    unit, hop_time, lead = 5.6 / chunks, 3.3, 12.0
+    unit, hop_time, lead = 5.6 / chunks, 3.3, 13.0
     inner_late, outer_late, gather_late, first_late = 1.0, 0.0, 1.5, 0.0
     hold = 0
     feed_first, feed_step = 10.0, 11.2 / chunks
@@ -991,6 +999,19 @@
                     come = inner + hop_time + gather_late
                 when = come + (t - j - 1) * hop_time
                 events.append((1000.0 + when if t == last else when, gather, (q, t, j)))
+
+    def masks_outer():
+        @pl.when((me == 0) | (me == last))
+        def _():
+            lax.fori_loop(0, blks, mask_step, 0)
+
+    def masks_inner():
+        @pl.when((me > 0) & (me < last))
+        def _():
+            lax.fori_loop(0, blks, mask_step, 0)
+
+    events.append((feed_first + feed_step * (chunks - 1) + 0.1, masks_outer, ()))
+    events.append((999.0, masks_inner, ()))
     events.sort(key=lambda e: e[0])
     for _, step, taken in events:
         step(*taken)
@@ -1018,7 +1039,7 @@
                 left(rise_send, kv.at[pl.ds(0, blks * rows * (t + 1)), sent_cols])
             if t > 0:
                 left(down_last_send, down_last)
-                left(fall_send, kv.at[pl.ds(0, blks * rows * (sp - t)), sent_cols])
+                left(fall_send, kv.at[pl.ds(0, (blks - 1) * rows * (sp - t)), sent_cols])
 
     landed(o_recv, obuf.at[some])
     left(o_send, obuf.at[some])
@@ -1068,7 +1089,7 @@
             pltpu.VMEM((blks, cut, pair), F32),
             pltpu.VMEM((blks, rows, HEAD), F32),
             pltpu.VMEM((blks, rows, HEAD), F32),
-            pltpu.VMEM((rows, 2 * span + rows), F32),
+            pltpu.VMEM((blks, rows, 2 * span + rows), F32),
             dma((chunks + 2 * blks + 1,)),
             dma,
             by_sp,

time: 60 us -> 57.7 us (0.962)
  Pallas kernels: 59 us -> 56.7 us
    pallas_call x1, Pallas kernels: 59 us -> 56.7 us  [heads_call(): pl.pallas_call(functools.partial(heads_kernel, (sp, blks, reps, rows, chu...]
where the time goes in v3:
time: 57.7 us; the launch traced here: 57.5 us
  Pallas kernels  56.7 us (98%)
  local copies, waits for them, and re-layouts  0.8 us (1%)
    pallas_call x1, Pallas kernels, heads_call(): pl.pallas_call(functools.partial(heads_kernel, (sp, blks, reps, rows, chu...  56.7 us

profile of v3, /device:TPU:0, one launch (start us, length us, event | category | flops | bytes accessed | tf_op | source)
XLA Modules:
  0.0 57.5 jit_solution(9045218971179996401)
XLA Ops:
  0.0 56.7 %masked_attention.1 = bf16[1,128,2048]{2,1,0:T(8,128)(2,1)S(1)} custom-call(bf16[1,128,4096]{2,1,0:T(8,128)(2,1)} %hidden_ref.1, bf16[1,128,2048]{2,1,0:T(8,128)(2,1)} %queries_ref.1, f32[1,4096]{1,0:T(1,128)} %bitcast.1, bf16[1024,512]{1,0:T(8,128)(2,1)} %kw_ref.1, bf16[1024,512]{1,0:T(8,128)(2,1)} %vw_ref.1, bf16[512]{0:T(512)(128)(2,1)} %kb_ref.1, ...), custom_call_target="tpu_custom_call" | custom-call | tf_op jit(solution)/shard_map/masked_attention/pallas_call | solution.py:1067
  56.7 0.8 %copy.10 = bf16[1,128,2048]{2,1,0:T(8,128)(2,1)} copy(bf16[1,128,2048]{2,1,0:T(8,128)(2,1)S(1)} %masked_attention.1) | data formatting | bytes 1048576

commit v4 on v3

--- a/solution.py
+++ b/solution.py
@@ -957,7 +957,7 @@
         return carry
 
     unit, hop_time, lead = 5.6 / chunks, 3.3, 13.0
-    inner_late, outer_late, gather_late, first_late = 1.0, 0.0, 1.5, 0.0
+    inner_late, outer_late, gather_late, first_late = 1.0, 0.0, 4.0, 0.0
     hold = 0
     feed_first, feed_step = 10.0, 11.2 / chunks
     queue = []

time: 57.7 us -> 57.5 us (level)
  no operation moved by 1% of the time
where the time goes in v4:
time: 57.5 us; the launch traced here: 57.3 us
  Pallas kernels  56.5 us (98%)
  local copies, waits for them, and re-layouts  0.8 us (1%)
    pallas_call x1, Pallas kernels, heads_call(): pl.pallas_call(functools.partial(heads_kernel, (sp, blks, reps, rows, chu...  56.5 us

profile of v4, /device:TPU:0, one launch (start us, length us, event | category | flops | bytes accessed | tf_op | source)
XLA Modules:
  0.0 57.3 jit_solution(8124107928023056027)
XLA Ops:
  0.0 56.5 %masked_attention.1 = bf16[1,128,2048]{2,1,0:T(8,128)(2,1)S(1)} custom-call(bf16[1,128,4096]{2,1,0:T(8,128)(2,1)} %hidden_ref.1, bf16[1,128,2048]{2,1,0:T(8,128)(2,1)} %queries_ref.1, f32[1,4096]{1,0:T(1,128)} %bitcast.1, bf16[1024,512]{1,0:T(8,128)(2,1)} %kw_ref.1, bf16[1024,512]{1,0:T(8,128)(2,1)} %vw_ref.1, bf16[512]{0:T(512)(128)(2,1)} %kb_ref.1, ...), custom_call_target="tpu_custom_call" | custom-call | tf_op jit(solution)/shard_map/masked_attention/pallas_call | solution.py:1067
  56.5 0.8 %copy.10 = bf16[1,128,2048]{2,1,0:T(8,128)(2,1)} copy(bf16[1,128,2048]{2,1,0:T(8,128)(2,1)S(1)} %masked_attention.1) | data formatting | bytes 1048576
